TPU v7x, 32 devices: a whole 2x2x4 slice. The times are simulated.
32 devices in a mesh: grp: 4 (over z), row: 4 (over y, core), col: 2 (over x).
Axes of the slice: x: 2, y: 2, z: 4, core: 2. Of those that a mesh axis runs over, the one named last changes fastest.
Arguments:
- tokens: bfloat16 [2048, 4608], P(('grp', 'row', 'col')), parts along dimension 0, may hold values from -6 to 6
- ln_gain: float32 [4608], replicated, may hold values from 0.1 to 1.9
- w_in: bfloat16 [4608, 12288], P('row', 'col'), may hold values from -0.09375 to 0.09375
- b_in: float32 [12288], P('col'), may hold values from -3 to 3
- w_out: bfloat16 [12288, 4608], P('col', 'row'), may hold values from -0.0546875 to 0.0546875
- b_out: float32 [4608], P('row'), may hold values from -3 to 3
Outputs:
- result: bfloat16 [2048, 4608], P(('grp', 'row', 'col')), parts along dimension 0
There are 4 independent parts, one for each index of `grp`. A program takes and returns all parts, laid end to end along the dimension named above; an argument that names none is the same for every part. Nothing has to cross between parts.
All inputs are finite; a program needn't handle non-finite values.
Results may differ from a plain program's by a relative error of at most 0.0095.
Values may be sent and summed in bfloat16 or wider, within the bound.
A program may use at most 128 MiB of HBM per device.

v0:
```python
import jax
import jax.numpy as jnp
from jax import lax
from jax.experimental import pallas as pl
from jax.experimental.pallas import tpu as pltpu
from jax.sharding import PartitionSpec as P

MESH = pl.DeviceIdType.MESH
F32, BF16 = jnp.float32, jnp.bfloat16


QUARTERS = (0, 1, 2, 3, 4)
CHUNKS = (((0, 0),), ((1, 0), (0, 1)), ((1, 1), (1, 2)), ((0, 2), (1, 3)), ((0, 3),))
SLICES = ((1, 1, 2, 2), (3, 3), (3, 3), (3, 3), (2, 2, 2))


def plan(rows):
    spans = [(rows * a // 4, rows * b // 4) for a, b in zip(QUARTERS, QUARTERS[1:])]
    base, starts, at = {}, [], 0
    for chunk in CHUNKS:
        starts.append(at)
        for cc, s in chunk:
            base[cc, s] = at
            at += 4 * (spans[s][1] - spans[s][0])
    return spans, base, starts, [b - a for a, b in zip(starts, starts[1:] + [at])]


def tile_of(size, limit):
    return next(t for t in range(limit, 0, -128) if size % t == 0)


def block_kernel(
    tokens_hbm, gain_hbm, w_in_hbm, b_in_hbm, w_out_hbm, b_out_hbm, out_ref,
    tokens, gain_ref, b_in_ref, b_out_ref, gain, b_in, b_out, w_in, w_out, normed, panel, psend, precv, ssend, srecv, hidden, total,
    okeep, osend, orecv, branch, regrouped,
    v_sem, t_sem, w_sem, send_sem, in_recv, fwd_recv, p_recv, s_recv, h_recv, o_recv, b_recv,
):
    r, c = lax.axis_index("row"), lax.axis_index("col")
    y, k = r // 2, r % 2
    partner, across, diagonal = 2 * y + (1 - k), 2 * (1 - y) + k, 2 * (1 - y) + (1 - k)
    others = (across, diagonal, partner)
    rows, width = tokens.shape
    depth = w_in.shape[0]
    tiles, _, tile = psend.shape
    half = tiles * tile
    spans, base, starts, counts = plan(rows)
    scope = jax.named_scope

    def tall(s):
        return spans[s][1] - spans[s][0]

    def span(s):
        return pl.ds(spans[s][0], tall(s))

    def quads(s):
        return pl.ds(4 * spans[s][0], 4 * tall(s))

    def order(j, i):
        return sum(len(cuts) for cuts in SLICES[:j]) + i

    def part(first, s, q):
        return pl.ds(pl.multiple_of(first + q * tall(s), 8), tall(s))

    def flat(j):
        return pl.ds(starts[j], counts[j])

    def bounds(j, i):
        return tiles * sum(SLICES[j][:i]) // 6, tiles * sum(SLICES[j][: i + 1]) // 6

    def cut(j, i):
        lo, hi = bounds(j, i)
        return pl.ds(lo, hi - lo)

    def remote(src, dst, send, recv, row, col=None):
        target = {"row": row} if col is None else {"row": row, "col": col}
        return pltpu.make_async_remote_copy(
            src_ref=src, dst_ref=dst, send_sem=send, recv_sem=recv, device_id=target, device_id_type=MESH
        )

    def load(which):
        return pltpu.make_async_copy((w_in_hbm, w_out_hbm)[which], (w_in, w_out)[which], w_sem.at[which])

    def fetch(s):
        return pltpu.make_async_copy(tokens_hbm.at[span(s)], tokens.at[span(s)], t_sem.at[s])

    barrier = pltpu.get_barrier_semaphore()
    for target in ({"row": across}, {"row": diagonal}, {"row": partner}, {"col": 1 - c}):
        pl.semaphore_signal(barrier, inc=1, device_id=target, device_id_type=MESH)
    def vector(i):
        src, dst = ((gain_hbm, gain_ref), (b_in_hbm, b_in_ref), (b_out_hbm, b_out_ref))[i]
        return pltpu.make_async_copy(src, dst, v_sem.at[i])

    fetch(0).start()
    vector(0).start()
    for s in range(1, len(spans)):
        fetch(s).start()
    load(0).start()
    vector(1).start()
    vector(2).start()

    def flatten(src, dst, begin, size):
        for i in range(size // 128):
            dst[:, i * 128 : (i + 1) * 128] = src[pl.ds(begin + i, 1), :]

    def normalize(s):
        values = tokens[span(s), :].astype(F32)
        centered = values - jnp.mean(values, axis=1, keepdims=True)
        var = jnp.mean(centered * centered, axis=1, keepdims=True)
        scaled = (centered * lax.rsqrt(var + 1e-06) * gain[...]).astype(BF16)
        for q in range(4):
            normed[q, span(s), :] = scaled[:, q * depth : (q + 1) * depth]

    def piece(s, i):
        return remote(
            normed.at[others[i], span(s)], panel.at[part(base[0, s], s, r)], send_sem.at[0], in_recv.at[s], others[i]
        )

    def forward(s):
        return remote(
            panel.at[pl.ds(base[0, s], 4 * tall(s))], panel.at[pl.ds(base[1, s], 4 * tall(s))],
            send_sem.at[1], fwd_recv.at[s], r, 1 - c,
        )

    def gathered(s):
        held = panel.at[pl.ds(base[0, s], 3 * tall(s))]
        remote(held, held, send_sem.at[0], in_recv.at[s], across).wait_recv()
        forward(s).start()

    def share(j, i):
        return remote(
            psend.at[cut(j, i), flat(j)], precv.at[cut(j, i), flat(j)], send_sem.at[2], p_recv.at[order(j, i)], partner
        )

    def cross(j, i):
        return remote(
            ssend.at[cut(j, i), flat(j)], srecv.at[cut(j, i), flat(j)], send_sem.at[3], s_recv.at[order(j, i)], across
        )

    def spread(j, i, which):
        held = hidden.at[which, cut(j, i), flat(j)]
        return remote(held, held, send_sem.at[4], h_recv.at[order(j, i)], partner)

    def lend(s):
        return remote(osend.at[quads(s)], orecv.at[quads(s)], send_sem.at[5], o_recv.at[s], r, 1 - c)

    def give(s, i):
        q = others[i]
        return remote(
            branch.at[part(4 * spans[s][0], s, q)], regrouped.at[r, span(s)], send_sem.at[6], b_recv.at[s], q
        )

    def each_tile(j, i, body):
        lo, hi = bounds(j, i)
        if hi - lo == 1:
            body(lo)
        else:
            pl.loop(lo, hi)(body)

    def first(j, between=()):
        def columns(core, t):
            return pl.ds(pl.multiple_of(core * half + t * tile, tile), tile)

        def theirs(i):
            def one(t):
                x = panel[flat(j), :]
                psend[t, flat(j), :] = jnp.dot(
                    x, w_in[:, columns(1 - k, t)], preferred_element_type=F32
                ).astype(BF16)

            with scope(f"theirs{j}"):
                each_tile(j, i, one)
            share(j, i).start()

        def ours(i):
            with scope(f"sharewait{j}"):
                share(j, i).wait_recv()

            def one(t):
                x = panel[flat(j), :]
                mine = jnp.dot(x, w_in[:, columns(k, t)], preferred_element_type=F32)
                ssend[t, flat(j), :] = (mine + precv[t, flat(j), :].astype(F32)).astype(BF16)

            with scope(f"ours{j}"):
                each_tile(j, i, one)
            cross(j, i).start()

        count = len(SLICES[j])
        theirs(0)
        for s in between:
            gathered(s)
        for i in range(count):
            if i + 1 < count:
                theirs(i + 1)
            ours(i)

    def second(j):
        acc = total.at[pl.ds(0, counts[j])]
        acc[...] = jnp.zeros((counts[j], depth), F32)
        count = len(SLICES[j])

        def down(i, which):
            def one(t):
                deep = pl.ds(pl.multiple_of(which * half + t * tile, tile), tile)
                acc[...] += jnp.dot(hidden[which, t, flat(j), :], w_out[deep, :], preferred_element_type=F32)

            with scope(f"down{j}"):
                each_tile(j, i, one)

        def theirs(i):
            with scope(f"spreadwait{j}"):
                spread(j, i, 1 - k).wait_recv()
            down(i, 1 - k)

        for i in range(count):
            with scope(f"crosswait{j}"):
                cross(j, i).wait_recv()

            def activate(t):
                bias = b_in[:, pl.ds(pl.multiple_of(t * tile, tile), tile)]
                v = ssend[t, flat(j), :].astype(F32) + srecv[t, flat(j), :].astype(F32) + bias
                hidden[k, t, flat(j), :] = (v * (1.0 + lax.erf(v * (0.5**0.5))) * 0.5).astype(BF16)

            with scope(f"gelu{j}"):
                each_tile(j, i, activate)
            spread(j, i, k).start()
            if j == 0 and i == 0:
                load(1).wait()
            down(i, k)
            if i > 0:
                theirs(i - 1)
        theirs(count - 1)
        for cc, s in sorted(CHUNKS[j], reverse=True):
            held = total[pl.ds(base[cc, s] - starts[j], 4 * tall(s)), :]
            if cc == 0:
                okeep[quads(s), :] = held
            else:
                osend[quads(s), :] = held.astype(BF16)
                lend(s).start()

    def finish(s):
        with scope(f"lendwait{s}"):
            lend(s).wait_recv()
        summed = okeep[quads(s), :] + orecv[quads(s), :].astype(F32) + b_out[...]
        branch[quads(s), :] = summed.astype(BF16)
        for i in range(3):
            give(s, i).start()
        regrouped[r, span(s), :] = branch[part(4 * spans[s][0], s, r), :]

    def settle(s):
        with scope(f"givewait{s}"):
            held = branch.at[pl.ds(0, 3 * tall(s))]
            remote(held, held, send_sem.at[6], b_recv.at[s], across).wait_recv()
        for q in range(4):
            out_ref[span(s), q * depth : (q + 1) * depth] = regrouped[q, span(s), :]

    vector(0).wait()
    flatten(gain_ref, gain, 0, width)
    for s in range(len(spans)):
        with scope(f"fetch{s}"):
            fetch(s).wait()
        with scope(f"norm{s}"):
            normalize(s)
        if s == 0:
            with scope("barrier"):
                pl.semaphore_wait(barrier, 4)
        for i in range(3):
            piece(s, i).start()
        panel[part(base[0, s], s, r), :] = normed[r, span(s), :]

    with scope("inwait0"):
        gathered(0)
    with scope("loadw"):
        load(0).wait()
    load(1).start()
    first(0)
    with scope("inwait1"):
        gathered(1)
    with scope("fwdwait0"):
        forward(0).wait_recv()
    first(1, between=(2, 3))
    with scope("fwdwait1"):
        forward(1).wait_recv()
    with scope("fwdwait2"):
        forward(2).wait_recv()
    first(2)
    with scope("fwdwait3"):
        forward(3).wait_recv()
    first(3)
    first(4)

    vector(1).wait()
    flatten(b_in_ref, b_in, k * (half // 128), half)
    vector(2).wait()
    flatten(b_out_ref, b_out, 0, depth)
    second(0)
    second(1)
    finish(0)
    second(2)
    finish(1)
    second(3)
    finish(2)
    second(4)
    finish(3)
    for s in range(len(spans)):
        settle(s)

    with scope("drain"):
        sent = (
            normed.at[pl.ds(0, 3)], panel.at[pl.ds(0, 4 * rows)], psend, ssend, hidden.at[k], osend,
            branch.at[pl.ds(0, 3 * rows)],
        )
        for i, held in enumerate(sent):
            remote(held, held, send_sem.at[i], send_sem.at[i], across).wait_send()


def fused(tokens, ln_gain, w_in, b_in, w_out, b_out):
    rows, width = tokens.shape
    depth, units = w_in.shape
    half = units // 2
    tile = tile_of(half, 512)
    spans, _, _, counts = plan(rows)
    many, cuts = len(spans), sum(len(cuts) for cuts in SLICES)
    vmem, dma = pltpu.VMEM, pltpu.SemaphoreType.DMA
    in_vmem, in_hbm = pl.BlockSpec(memory_space=vmem), pl.BlockSpec(memory_space=pl.ANY)
    stage = vmem((half // tile, 8 * rows, tile), BF16)
    branch_out = pl.pallas_call(
        block_kernel,
        out_shape=pltpu.VMEM((rows, width), BF16),
        in_specs=[in_hbm] * 6,
        out_specs=in_vmem,
        scratch_shapes=[
            vmem((rows, width), BF16),
            vmem((width // 128, 128), F32),
            vmem((units // 128, 128), F32),
            vmem((depth // 128, 128), F32),
            vmem((1, width), F32),
            vmem((1, half), F32),
            vmem((1, depth), F32),
            vmem(w_in.shape, BF16),
            vmem(w_out.shape, BF16),
            vmem((4, rows, depth), BF16),
            vmem((8 * rows, depth), BF16),
            stage,
            stage,
            stage,
            stage,
            vmem((2, half // tile, 8 * rows, tile), BF16),
            vmem((max(counts), depth), F32),
            vmem((4 * rows, depth), F32),
            vmem((4 * rows, depth), BF16),
            vmem((4 * rows, depth), BF16),
            vmem((4 * rows, depth), BF16),
            vmem((4, rows, depth), BF16),
            dma((3,)),
            dma((many,)),
            dma((2,)),
            dma((7,)),
            dma((many,)),
            dma((many,)),
            dma((cuts,)),
            dma((cuts,)),
            dma((cuts,)),
            dma((many,)),
            dma((many,)),
        ],
        compiler_params=pltpu.CompilerParams(
            collective_id=0, has_side_effects=True, vmem_limit_bytes=62000000
        ),
        name="mlp_block",
    )(tokens, ln_gain.reshape(-1, 128), w_in, b_in.reshape(-1, 128), w_out, b_out.reshape(-1, 128))
    return (tokens.astype(F32) + branch_out.astype(F32)).astype(BF16)


def local(tokens, ln_gain, w_in, b_in, w_out, b_out):
    values = tokens.astype(jnp.float32)
    row_mean = jnp.mean(values, axis=1, keepdims=True)
    centered = values - row_mean
    row_var = jnp.mean(centered * centered, axis=1, keepdims=True)
    normed = (centered * lax.rsqrt(row_var + 1e-06) * ln_gain).astype(jnp.bfloat16)
    own_cols = lax.all_to_all(normed, "row", split_axis=1, concat_axis=0, tiled=True)
    partial_pre = jnp.dot(
        lax.all_gather(own_cols, "col", axis=0, tiled=True),
        w_in,
        preferred_element_type=jnp.float32,
    )
    preact = lax.psum_scatter(partial_pre, "row", scatter_dimension=0, tiled=True) + b_in
    hidden = jax.nn.gelu(preact, approximate=False).astype(jnp.bfloat16)
    down_part = jnp.dot(
        lax.all_gather(hidden, "row", axis=0, tiled=True), w_out, preferred_element_type=jnp.float32
    )
    summed = lax.psum_scatter(
        down_part.astype(jnp.bfloat16), "col", scatter_dimension=0, tiled=True
    ).astype(jnp.float32)
    branch_out = (summed + b_out).astype(jnp.bfloat16)
    regrouped = lax.all_to_all(branch_out, "row", split_axis=0, concat_axis=1, tiled=True)
    return (values + regrouped.astype(jnp.float32)).astype(jnp.bfloat16)


def solution(mesh):
    in_specs = (
        P(("grp", "row", "col"), None),
        P(),
        P("row", "col"),
        P("col"),
        P("col", "row"),
        P("row"),
    )
    out_specs = P(("grp", "row", "col"), None)
    body = fused if (mesh.shape["row"], mesh.shape["col"]) == (4, 2) else local
    return jax.shard_map(body, mesh=mesh, in_specs=in_specs, out_specs=out_specs, check_vma=False)
```

profile of v0, /device:TPU:0, one launch (start us, length us, event | category | flops | bytes accessed | tf_op | source)
XLA Modules:
  0.0 86.2 jit_solution(586098719367773845)
XLA Ops:
  0.0 0.0 copy-start
  0.0 85.2 %mlp_block.1 = bf16[64,4608]{1,0:T(8,128)(2,1)S(1)} custom-call(bf16[64,4608]{1,0:T(8,128)(2,1)} %tokens_hbm.1, f32[36,128]{1,0:T(8,128)} %bitcast.4, bf16[1152,6144]{1,0:T(8,128)(2,1)} %w_in_hbm.1, f32[48,128]{1,0:T(8,128)} %bitcast.3, bf16[6144,1152]{1,0:T(8,128)(2,1)} %w_out_hbm.1, f32[9,128]{1,0:T(8,128)} %bitcast.5), custom_call_target="tpu_custom_call" | custom-call | tf_op jit(solution)/shard_map/mlp_block/pallas_call | solution.py:326
  85.3 0.0 copy-done
  85.3 1.0 %add_convert_fusion = bf16[64,4608]{1,0:T(8,128)(2,1)} fusion(bf16[64,4608]{1,0:T(8,128)(2,1)S(1)} %mlp_block.1, bf16[64,4608]{1,0:T(8,128)(2,1)S(1)} %copy-done), kind=kLoop, calls=%fused_computation | loop fusion | flops 1179648 | bytes 1769472 | tf_op jit(solution)/shard_map/convert_element_type | solution.py:371
Async XLA Ops:
  0.0 85.3 %copy-start = (bf16[64,4608]{1,0:T(8,128)(2,1)S(1)}, bf16[64,4608]{1,0:T(8,128)(2,1)}, u32[]{:S(2)}) copy-start(bf16[64,4608]{1,0:T(8,128)(2,1)} %tokens_hbm.1) | copy-start | bytes 1769476
where the time goes:
time: 86.4 us; the launch traced here: 86.2 us
  Pallas kernels  85.2 us (99%)
  other arithmetic  0.95 us (1%)
    pallas_call x1, Pallas kernels, fused(): pl.pallas_call(block_kernel, out_shape=pltpu.VMEM((rows, width), BF16), i...  85.2 us

commit v1 on v0

--- a/solution.py
+++ b/solution.py
@@ -12,6 +12,7 @@
 QUARTERS = (0, 1, 2, 3, 4)
 CHUNKS = (((0, 0),), ((1, 0), (0, 1)), ((1, 1), (1, 2)), ((0, 2), (1, 3)), ((0, 3),))
 SLICES = ((1, 1, 2, 2), (3, 3), (3, 3), (3, 3), (2, 2, 2))
+TAKEN = ((6,), (6,), (6,), (3, 3), (2, 2, 2))
 
 
 def plan(rows):
@@ -55,21 +56,25 @@
     def quads(s):
         return pl.ds(4 * spans[s][0], 4 * tall(s))
 
-    def order(j, i):
-        return sum(len(cuts) for cuts in SLICES[:j]) + i
-
     def part(first, s, q):
         return pl.ds(pl.multiple_of(first + q * tall(s), 8), tall(s))
 
     def flat(j):
         return pl.ds(starts[j], counts[j])
 
-    def bounds(j, i):
-        return tiles * sum(SLICES[j][:i]) // 6, tiles * sum(SLICES[j][: i + 1]) // 6
-
-    def cut(j, i):
-        lo, hi = bounds(j, i)
+    def bounds(slices, j, i):
+        return tiles * sum(slices[j][:i]) // 6, tiles * sum(slices[j][: i + 1]) // 6
+
+    def cut(slices, j, i):
+        lo, hi = bounds(slices, j, i)
         return pl.ds(lo, hi - lo)
+
+    def order(slices, j, i):
+        return sum(len(cuts) for cuts in slices[:j]) + i
+
+    def taken(j, i):
+        lo = bounds(SLICES, j, i)[0]
+        return next(n for n in range(len(TAKEN[j])) if lo < bounds(TAKEN, j, n)[1])
 
     def remote(src, dst, send, recv, row, col=None):
         target = {"row": row} if col is None else {"row": row, "col": col}
@@ -80,8 +85,9 @@
     def load(which):
         return pltpu.make_async_copy((w_in_hbm, w_out_hbm)[which], (w_in, w_out)[which], w_sem.at[which])
 
-    def fetch(s):
-        return pltpu.make_async_copy(tokens_hbm.at[span(s)], tokens.at[span(s)], t_sem.at[s])
+    def fetch(i):
+        at = (span(0), pl.ds(spans[0][1], rows - spans[0][1]))[i]
+        return pltpu.make_async_copy(tokens_hbm.at[at], tokens.at[at], t_sem.at[i])
 
     barrier = pltpu.get_barrier_semaphore()
     for target in ({"row": across}, {"row": diagonal}, {"row": partner}, {"col": 1 - c}):
@@ -92,8 +98,7 @@
 
     fetch(0).start()
     vector(0).start()
-    for s in range(1, len(spans)):
-        fetch(s).start()
+    fetch(1).start()
     load(0).start()
     vector(1).start()
     vector(2).start()
@@ -127,18 +132,16 @@
         forward(s).start()
 
     def share(j, i):
-        return remote(
-            psend.at[cut(j, i), flat(j)], precv.at[cut(j, i), flat(j)], send_sem.at[2], p_recv.at[order(j, i)], partner
-        )
-
-    def cross(j, i):
-        return remote(
-            ssend.at[cut(j, i), flat(j)], srecv.at[cut(j, i), flat(j)], send_sem.at[3], s_recv.at[order(j, i)], across
-        )
+        at = (cut(SLICES, j, i), flat(j))
+        return remote(psend.at[at], precv.at[at], send_sem.at[2], p_recv.at[order(SLICES, j, i) % 4], partner)
+
+    def cross(j, at, n):
+        at = (at, flat(j))
+        return remote(ssend.at[at], srecv.at[at], send_sem.at[3], s_recv.at[order(TAKEN, j, n)], across)
 
     def spread(j, i, which):
-        held = hidden.at[which, cut(j, i), flat(j)]
-        return remote(held, held, send_sem.at[4], h_recv.at[order(j, i)], partner)
+        held = hidden.at[which, cut(TAKEN, j, i), flat(j)]
+        return remote(held, held, send_sem.at[4], h_recv.at[order(TAKEN, j, i)], partner)
 
     def lend(s):
         return remote(osend.at[quads(s)], orecv.at[quads(s)], send_sem.at[5], o_recv.at[s], r, 1 - c)
@@ -149,8 +152,8 @@
             branch.at[part(4 * spans[s][0], s, q)], regrouped.at[r, span(s)], send_sem.at[6], b_recv.at[s], q
         )
 
-    def each_tile(j, i, body):
-        lo, hi = bounds(j, i)
+    def each_tile(slices, j, i, body):
+        lo, hi = bounds(slices, j, i)
         if hi - lo == 1:
             body(lo)
         else:
@@ -168,7 +171,7 @@
                 ).astype(BF16)
 
             with scope(f"theirs{j}"):
-                each_tile(j, i, one)
+                each_tile(SLICES, j, i, one)
             share(j, i).start()
 
         def ours(i):
@@ -181,8 +184,8 @@
                 ssend[t, flat(j), :] = (mine + precv[t, flat(j), :].astype(F32)).astype(BF16)
 
             with scope(f"ours{j}"):
-                each_tile(j, i, one)
-            cross(j, i).start()
+                each_tile(SLICES, j, i, one)
+            cross(j, cut(SLICES, j, i), taken(j, i)).start()
 
         count = len(SLICES[j])
         theirs(0)
@@ -196,7 +199,7 @@
     def second(j):
         acc = total.at[pl.ds(0, counts[j])]
         acc[...] = jnp.zeros((counts[j], depth), F32)
-        count = len(SLICES[j])
+        count = len(TAKEN[j])
 
         def down(i, which):
             def one(t):
@@ -204,7 +207,7 @@
                 acc[...] += jnp.dot(hidden[which, t, flat(j), :], w_out[deep, :], preferred_element_type=F32)
 
             with scope(f"down{j}"):
-                each_tile(j, i, one)
+                each_tile(TAKEN, j, i, one)
 
         def theirs(i):
             with scope(f"spreadwait{j}"):
@@ -213,7 +216,7 @@
 
         for i in range(count):
             with scope(f"crosswait{j}"):
-                cross(j, i).wait_recv()
+                cross(j, cut(TAKEN, j, i), i).wait_recv()
 
             def activate(t):
                 bias = b_in[:, pl.ds(pl.multiple_of(t * tile, tile), tile)]
@@ -221,7 +224,7 @@
                 hidden[k, t, flat(j), :] = (v * (1.0 + lax.erf(v * (0.5**0.5))) * 0.5).astype(BF16)
 
             with scope(f"gelu{j}"):
-                each_tile(j, i, activate)
+                each_tile(TAKEN, j, i, activate)
             spread(j, i, k).start()
             if j == 0 and i == 0:
                 load(1).wait()
@@ -251,13 +254,17 @@
             held = branch.at[pl.ds(0, 3 * tall(s))]
             remote(held, held, send_sem.at[6], b_recv.at[s], across).wait_recv()
         for q in range(4):
-            out_ref[span(s), q * depth : (q + 1) * depth] = regrouped[q, span(s), :]
+            at = pl.ds(q * depth, depth)
+            out_ref[span(s), at] = (
+                tokens[span(s), at].astype(F32) + regrouped[q, span(s), :].astype(F32)
+            ).astype(BF16)
 
     vector(0).wait()
     flatten(gain_ref, gain, 0, width)
     for s in range(len(spans)):
-        with scope(f"fetch{s}"):
-            fetch(s).wait()
+        if s < 2:
+            with scope(f"fetch{s}"):
+                fetch(s).wait()
         with scope(f"norm{s}"):
             normalize(s)
         if s == 0:
@@ -319,11 +326,11 @@
     half = units // 2
     tile = tile_of(half, 512)
     spans, _, _, counts = plan(rows)
-    many, cuts = len(spans), sum(len(cuts) for cuts in SLICES)
+    many, cuts = len(spans), sum(len(slices) for slices in TAKEN)
     vmem, dma = pltpu.VMEM, pltpu.SemaphoreType.DMA
     in_vmem, in_hbm = pl.BlockSpec(memory_space=vmem), pl.BlockSpec(memory_space=pl.ANY)
     stage = vmem((half // tile, 8 * rows, tile), BF16)
-    branch_out = pl.pallas_call(
+    return pl.pallas_call(
         block_kernel,
         out_shape=pltpu.VMEM((rows, width), BF16),
         in_specs=[in_hbm] * 6,
@@ -352,12 +359,12 @@
             vmem((4 * rows, depth), BF16),
             vmem((4, rows, depth), BF16),
             dma((3,)),
-            dma((many,)),
+            dma((2,)),
             dma((2,)),
             dma((7,)),
             dma((many,)),
             dma((many,)),
-            dma((cuts,)),
+            dma((4,)),
             dma((cuts,)),
             dma((cuts,)),
             dma((many,)),
@@ -368,7 +375,6 @@
         ),
         name="mlp_block",
     )(tokens, ln_gain.reshape(-1, 128), w_in, b_in.reshape(-1, 128), w_out, b_out.reshape(-1, 128))
-    return (tokens.astype(F32) + branch_out.astype(F32)).astype(BF16)
 
 
 def local(tokens, ln_gain, w_in, b_in, w_out, b_out):

time: 86.4 us -> 86 us (level)
  other arithmetic: 0.95 us -> 0 us
    convert_element_type x1 -> x0, other arithmetic: 0.95 us -> none  [fused(): return (tokens.astype(F32) + branch_out.astype(F32)).astype(BF16)]
where the time goes in v1:
time: 86 us; the launch traced here: 85.9 us
  Pallas kernels  85 us (99%)
    pallas_call x1, Pallas kernels, fused(): pl.pallas_call(block_kernel, out_shape=pltpu.VMEM((rows, width), BF16), i...  85 us

profile of v1, /device:TPU:0, one launch (start us, length us, event | category | flops | bytes accessed | tf_op | source)
XLA Modules:
  0.0 85.9 jit_solution(4097065210786800601)
XLA Ops:
  0.0 85.0 %mlp_block.1 = bf16[64,4608]{1,0:T(8,128)(2,1)S(1)} custom-call(bf16[64,4608]{1,0:T(8,128)(2,1)} %tokens_hbm.1, f32[36,128]{1,0:T(8,128)} %bitcast.4, bf16[1152,6144]{1,0:T(8,128)(2,1)} %w_in_hbm.1, f32[48,128]{1,0:T(8,128)} %bitcast.3, bf16[6144,1152]{1,0:T(8,128)(2,1)} %w_out_hbm.1, f32[9,128]{1,0:T(8,128)} %bitcast.5), custom_call_target="tpu_custom_call" | custom-call | tf_op jit(solution)/shard_map/mlp_block/pallas_call | solution.py:333
  85.0 0.8 copy.8

commit v2 on v1

--- a/solution.py
+++ b/solution.py
@@ -12,6 +12,7 @@
 QUARTERS = (0, 1, 2, 3, 4)
 CHUNKS = (((0, 0),), ((1, 0), (0, 1)), ((1, 1), (1, 2)), ((0, 2), (1, 3)), ((0, 3),))
 SLICES = ((1, 1, 2, 2), (3, 3), (3, 3), (3, 3), (2, 2, 2))
+PAIRED = (0, 1, 1, 2)
 TAKEN = ((6,), (6,), (6,), (3, 3), (2, 2, 2))
 
 
@@ -34,17 +35,18 @@
     tokens_hbm, gain_hbm, w_in_hbm, b_in_hbm, w_out_hbm, b_out_hbm, out_ref,
     tokens, gain_ref, b_in_ref, b_out_ref, gain, b_in, b_out, w_in, w_out, normed, panel, psend, precv, ssend, srecv, hidden, total,
     okeep, osend, orecv, branch, regrouped,
-    v_sem, t_sem, w_sem, send_sem, in_recv, fwd_recv, p_recv, s_recv, h_recv, o_recv, b_recv,
+    v_sem, t_sem, w_sem, send_sem, in_recv, fwd_recv, p_recv, s_recv, h_recv, o_recv,
 ):
     r, c = lax.axis_index("row"), lax.axis_index("col")
     y, k = r // 2, r % 2
     partner, across, diagonal = 2 * y + (1 - k), 2 * (1 - y) + k, 2 * (1 - y) + (1 - k)
-    others = (across, diagonal, partner)
+    others = (2 * (1 - y), 2 * (1 - y) + 1, partner)
     rows, width = tokens.shape
     depth = w_in.shape[0]
     tiles, _, tile = psend.shape
     half = tiles * tile
     spans, base, starts, counts = plan(rows)
+    last = len(spans) - 1
     scope = jax.named_scope
 
     def tall(s):
@@ -83,7 +85,7 @@
         )
 
     def load(which):
-        return pltpu.make_async_copy((w_in_hbm, w_out_hbm)[which], (w_in, w_out)[which], w_sem.at[which])
+        return pltpu.make_async_copy((w_in_hbm, w_out_hbm)[which], (w_in, w_out)[which], w_sem)
 
     def fetch(i):
         at = (span(0), pl.ds(spans[0][1], rows - spans[0][1]))[i]
@@ -94,14 +96,12 @@
         pl.semaphore_signal(barrier, inc=1, device_id=target, device_id_type=MESH)
     def vector(i):
         src, dst = ((gain_hbm, gain_ref), (b_in_hbm, b_in_ref), (b_out_hbm, b_out_ref))[i]
-        return pltpu.make_async_copy(src, dst, v_sem.at[i])
+        return pltpu.make_async_copy(src, dst, v_sem)
 
     fetch(0).start()
     vector(0).start()
     fetch(1).start()
     load(0).start()
-    vector(1).start()
-    vector(2).start()
 
     def flatten(src, dst, begin, size):
         for i in range(size // 128):
@@ -117,19 +117,22 @@
 
     def piece(s, i):
         return remote(
-            normed.at[others[i], span(s)], panel.at[part(base[0, s], s, r)], send_sem.at[0], in_recv.at[s], others[i]
+            normed.at[others[i], span(s)], panel.at[part(base[0, s], s, r)], send_sem.at[0], in_recv.at[min(s, 1)], others[i]
         )
 
     def forward(s):
         return remote(
             panel.at[pl.ds(base[0, s], 4 * tall(s))], panel.at[pl.ds(base[1, s], 4 * tall(s))],
-            send_sem.at[1], fwd_recv.at[s], r, 1 - c,
+            send_sem.at[1], fwd_recv.at[PAIRED[s]], r, 1 - c,
         )
 
-    def gathered(s):
-        held = panel.at[pl.ds(base[0, s], 3 * tall(s))]
-        remote(held, held, send_sem.at[0], in_recv.at[s], across).wait_recv()
-        forward(s).start()
+    def gathered(which, count):
+        held = panel.at[pl.ds(0, 3 * count)]
+        remote(held, held, send_sem.at[0], in_recv.at[which], across).wait_recv()
+
+    def passed(sem, which, *among):
+        held = panel.at[pl.ds(0, 4 * sum(tall(s) for s in among))]
+        remote(held, held, send_sem.at[1], sem.at[which], r, 1 - c).wait_recv()
 
     def share(j, i):
         at = (cut(SLICES, j, i), flat(j))
@@ -137,19 +140,19 @@
 
     def cross(j, at, n):
         at = (at, flat(j))
-        return remote(ssend.at[at], srecv.at[at], send_sem.at[3], s_recv.at[order(TAKEN, j, n)], across)
+        return remote(ssend.at[at], srecv.at[at], send_sem.at[2], s_recv.at[order(TAKEN, j, n)], across)
 
     def spread(j, i, which):
         held = hidden.at[which, cut(TAKEN, j, i), flat(j)]
-        return remote(held, held, send_sem.at[4], h_recv.at[order(TAKEN, j, i)], partner)
+        return remote(held, held, send_sem.at[3], h_recv.at[order(TAKEN, j, i) % 4], partner)
 
     def lend(s):
-        return remote(osend.at[quads(s)], orecv.at[quads(s)], send_sem.at[5], o_recv.at[s], r, 1 - c)
+        return remote(osend.at[quads(s)], orecv.at[quads(s)], send_sem.at[1], o_recv.at[PAIRED[s]], r, 1 - c)
 
     def give(s, i):
         q = others[i]
         return remote(
-            branch.at[part(4 * spans[s][0], s, q)], regrouped.at[r, span(s)], send_sem.at[6], b_recv.at[s], q
+            branch.at[part(4 * spans[s][0], s, q)], regrouped.at[r, span(s)], send_sem.at[0], in_recv.at[s // last], q
         )
 
     def each_tile(slices, j, i, body):
@@ -159,7 +162,7 @@
         else:
             pl.loop(lo, hi)(body)
 
-    def first(j, between=()):
+    def first(j):
         def columns(core, t):
             return pl.ds(pl.multiple_of(core * half + t * tile, tile), tile)
 
@@ -189,8 +192,6 @@
 
         count = len(SLICES[j])
         theirs(0)
-        for s in between:
-            gathered(s)
         for i in range(count):
             if i + 1 < count:
                 theirs(i + 1)
@@ -241,8 +242,6 @@
                 lend(s).start()
 
     def finish(s):
-        with scope(f"lendwait{s}"):
-            lend(s).wait_recv()
         summed = okeep[quads(s), :] + orecv[quads(s), :].astype(F32) + b_out[...]
         branch[quads(s), :] = summed.astype(BF16)
         for i in range(3):
@@ -250,9 +249,6 @@
         regrouped[r, span(s), :] = branch[part(4 * spans[s][0], s, r), :]
 
     def settle(s):
-        with scope(f"givewait{s}"):
-            held = branch.at[pl.ds(0, 3 * tall(s))]
-            remote(held, held, send_sem.at[6], b_recv.at[s], across).wait_recv()
         for q in range(4):
             at = pl.ds(q * depth, depth)
             out_ref[span(s), at] = (
@@ -260,6 +256,7 @@
             ).astype(BF16)
 
     vector(0).wait()
+    vector(1).start()
     flatten(gain_ref, gain, 0, width)
     for s in range(len(spans)):
         if s < 2:
@@ -275,48 +272,57 @@
         panel[part(base[0, s], s, r), :] = normed[r, span(s), :]
 
     with scope("inwait0"):
-        gathered(0)
+        gathered(0, tall(0))
+    forward(0).start()
     with scope("loadw"):
         load(0).wait()
     load(1).start()
     first(0)
     with scope("inwait1"):
-        gathered(1)
+        gathered(1, rows - tall(0))
+    for s in range(1, last + 1):
+        forward(s).start()
     with scope("fwdwait0"):
-        forward(0).wait_recv()
-    first(1, between=(2, 3))
+        passed(fwd_recv, 0, 0)
+    first(1)
     with scope("fwdwait1"):
-        forward(1).wait_recv()
-    with scope("fwdwait2"):
-        forward(2).wait_recv()
+        passed(fwd_recv, 1, 1, 2)
     first(2)
     with scope("fwdwait3"):
-        forward(3).wait_recv()
+        passed(fwd_recv, 2, 3)
     first(3)
     first(4)
 
     vector(1).wait()
+    vector(2).start()
     flatten(b_in_ref, b_in, k * (half // 128), half)
+    second(0)
+    second(1)
     vector(2).wait()
     flatten(b_out_ref, b_out, 0, depth)
-    second(0)
-    second(1)
+    with scope("lendwait0"):
+        passed(o_recv, 0, 0)
     finish(0)
     second(2)
+    with scope("lendwait1"):
+        passed(o_recv, 1, 1, 2)
     finish(1)
     second(3)
     finish(2)
     second(4)
+    with scope("lendwait3"):
+        passed(o_recv, 2, 3)
     finish(3)
-    for s in range(len(spans)):
+    with scope("givewait0"):
+        gathered(0, rows - tall(last))
+    for s in range(last):
         settle(s)
+    with scope("givewait3"):
+        gathered(1, tall(last))
+    settle(last)
 
     with scope("drain"):
-        sent = (
-            normed.at[pl.ds(0, 3)], panel.at[pl.ds(0, 4 * rows)], psend, ssend, hidden.at[k], osend,
-            branch.at[pl.ds(0, 3 * rows)],
-        )
-        for i, held in enumerate(sent):
+        for i, held in enumerate((panel.at[pl.ds(0, 6 * rows)], panel, hidden, psend)):
             remote(held, held, send_sem.at[i], send_sem.at[i], across).wait_send()
 
 
@@ -326,7 +332,7 @@
     half = units // 2
     tile = tile_of(half, 512)
     spans, _, _, counts = plan(rows)
-    many, cuts = len(spans), sum(len(slices) for slices in TAKEN)
+    cuts = sum(len(slices) for slices in TAKEN)
     vmem, dma = pltpu.VMEM, pltpu.SemaphoreType.DMA
     in_vmem, in_hbm = pl.BlockSpec(memory_space=vmem), pl.BlockSpec(memory_space=pl.ANY)
     stage = vmem((half // tile, 8 * rows, tile), BF16)
@@ -358,17 +364,16 @@
             vmem((4 * rows, depth), BF16),
             vmem((4 * rows, depth), BF16),
             vmem((4, rows, depth), BF16),
+            dma,
+            dma((2,)),
+            dma,
+            dma((4,)),
+            dma((2,)),
             dma((3,)),
-            dma((2,)),
-            dma((2,)),
-            dma((7,)),
-            dma((many,)),
-            dma((many,)),
             dma((4,)),
             dma((cuts,)),
-            dma((cuts,)),
-            dma((many,)),
-            dma((many,)),
+            dma((4,)),
+            dma((3,)),
         ],
         compiler_params=pltpu.CompilerParams(
             collective_id=0, has_side_effects=True, vmem_limit_bytes=62000000

time: 86 us -> 85.8 us (level)
  no operation moved by 1% of the time
where the time goes in v2:
time: 85.8 us; the launch traced here: 85.7 us
  Pallas kernels  84.9 us (99%)
    pallas_call x1, Pallas kernels, fused(): pl.pallas_call(block_kernel, out_shape=pltpu.VMEM((rows, width), BF16), i...  84.9 us

profile of v2, /device:TPU:0, one launch (start us, length us, event | category | flops | bytes accessed | tf_op | source)
XLA Modules:
  0.0 85.7 jit_solution(9788591637724974919)
XLA Ops:
  0.0 84.9 %mlp_block.1 = bf16[64,4608]{1,0:T(8,128)(2,1)S(1)} custom-call(bf16[64,4608]{1,0:T(8,128)(2,1)} %tokens_hbm.1, f32[36,128]{1,0:T(8,128)} %bitcast.4, bf16[1152,6144]{1,0:T(8,128)(2,1)} %w_in_hbm.1, f32[48,128]{1,0:T(8,128)} %bitcast.3, bf16[6144,1152]{1,0:T(8,128)(2,1)} %w_out_hbm.1, f32[9,128]{1,0:T(8,128)} %bitcast.5), custom_call_target="tpu_custom_call" | custom-call | tf_op jit(solution)/shard_map/mlp_block/pallas_call | solution.py:339
  84.9 0.8 copy.8

commit v3 on v2

--- a/solution.py
+++ b/solution.py
@@ -12,7 +12,6 @@
 QUARTERS = (0, 1, 2, 3, 4)
 CHUNKS = (((0, 0),), ((1, 0), (0, 1)), ((1, 1), (1, 2)), ((0, 2), (1, 3)), ((0, 3),))
 SLICES = ((1, 1, 2, 2), (3, 3), (3, 3), (3, 3), (2, 2, 2))
-PAIRED = (0, 1, 1, 2)
 TAKEN = ((6,), (6,), (6,), (3, 3), (2, 2, 2))
 
 
@@ -35,7 +34,7 @@
     tokens_hbm, gain_hbm, w_in_hbm, b_in_hbm, w_out_hbm, b_out_hbm, out_ref,
     tokens, gain_ref, b_in_ref, b_out_ref, gain, b_in, b_out, w_in, w_out, normed, panel, psend, precv, ssend, srecv, hidden, total,
     okeep, osend, orecv, branch, regrouped,
-    v_sem, t_sem, w_sem, send_sem, in_recv, fwd_recv, p_recv, s_recv, h_recv, o_recv,
+    t_sem, w_sem, send_sem, in_recv, fwd_recv, p_recv, s_recv, h_recv, o_recv,
 ):
     r, c = lax.axis_index("row"), lax.axis_index("col")
     y, k = r // 2, r % 2
@@ -96,21 +95,26 @@
         pl.semaphore_signal(barrier, inc=1, device_id=target, device_id_type=MESH)
     def vector(i):
         src, dst = ((gain_hbm, gain_ref), (b_in_hbm, b_in_ref), (b_out_hbm, b_out_ref))[i]
-        return pltpu.make_async_copy(src, dst, v_sem)
+        return pltpu.make_async_copy(src, dst, w_sem)
 
     fetch(0).start()
     vector(0).start()
     fetch(1).start()
-    load(0).start()
 
     def flatten(src, dst, begin, size):
         for i in range(size // 128):
             dst[:, i * 128 : (i + 1) * 128] = src[pl.ds(begin + i, 1), :]
 
+    def mean(x):
+        parts = [x[:, at : at + 128] for at in range(0, width, 128)]
+        while len(parts) > 1:
+            parts = [sum(parts[i + 1 : i + 2], parts[i]) for i in range(0, len(parts), 2)]
+        return jnp.sum(parts[0], axis=1, keepdims=True) * (1.0 / width)
+
     def normalize(s):
         values = tokens[span(s), :].astype(F32)
-        centered = values - jnp.mean(values, axis=1, keepdims=True)
-        var = jnp.mean(centered * centered, axis=1, keepdims=True)
+        centered = values - mean(values)
+        var = mean(centered * centered)
         scaled = (centered * lax.rsqrt(var + 1e-06) * gain[...]).astype(BF16)
         for q in range(4):
             normed[q, span(s), :] = scaled[:, q * depth : (q + 1) * depth]
@@ -123,7 +127,7 @@
     def forward(s):
         return remote(
             panel.at[pl.ds(base[0, s], 4 * tall(s))], panel.at[pl.ds(base[1, s], 4 * tall(s))],
-            send_sem.at[1], fwd_recv.at[PAIRED[s]], r, 1 - c,
+            send_sem.at[1], fwd_recv.at[min(s, 1)], r, 1 - c,
         )
 
     def gathered(which, count):
@@ -147,7 +151,7 @@
         return remote(held, held, send_sem.at[3], h_recv.at[order(TAKEN, j, i) % 4], partner)
 
     def lend(s):
-        return remote(osend.at[quads(s)], orecv.at[quads(s)], send_sem.at[1], o_recv.at[PAIRED[s]], r, 1 - c)
+        return remote(osend.at[quads(s)], orecv.at[quads(s)], send_sem.at[1], o_recv.at[s // last], r, 1 - c)
 
     def give(s, i):
         q = others[i]
@@ -229,6 +233,7 @@
             spread(j, i, k).start()
             if j == 0 and i == 0:
                 load(1).wait()
+                vector(2).start()
             down(i, k)
             if i > 0:
                 theirs(i - 1)
@@ -256,7 +261,7 @@
             ).astype(BF16)
 
     vector(0).wait()
-    vector(1).start()
+    load(0).start()
     flatten(gain_ref, gain, 0, width)
     for s in range(len(spans)):
         if s < 2:
@@ -276,8 +281,10 @@
     forward(0).start()
     with scope("loadw"):
         load(0).wait()
+    vector(1).start()
+    first(0)
+    vector(1).wait()
     load(1).start()
-    first(0)
     with scope("inwait1"):
         gathered(1, rows - tall(0))
     for s in range(1, last + 1):
@@ -286,32 +293,26 @@
         passed(fwd_recv, 0, 0)
     first(1)
     with scope("fwdwait1"):
-        passed(fwd_recv, 1, 1, 2)
+        passed(fwd_recv, 1, *range(1, last + 1))
     first(2)
-    with scope("fwdwait3"):
-        passed(fwd_recv, 2, 3)
     first(3)
     first(4)
 
-    vector(1).wait()
-    vector(2).start()
     flatten(b_in_ref, b_in, k * (half // 128), half)
     second(0)
     second(1)
     vector(2).wait()
     flatten(b_out_ref, b_out, 0, depth)
+    second(2)
     with scope("lendwait0"):
-        passed(o_recv, 0, 0)
+        passed(o_recv, 0, *range(last))
     finish(0)
-    second(2)
-    with scope("lendwait1"):
-        passed(o_recv, 1, 1, 2)
     finish(1)
     second(3)
     finish(2)
     second(4)
     with scope("lendwait3"):
-        passed(o_recv, 2, 3)
+        passed(o_recv, 1, last)
     finish(3)
     with scope("givewait0"):
         gathered(0, rows - tall(last))
@@ -364,16 +365,15 @@
             vmem((4 * rows, depth), BF16),
             vmem((4 * rows, depth), BF16),
             vmem((4, rows, depth), BF16),
-            dma,
             dma((2,)),
             dma,
             dma((4,)),
             dma((2,)),
-            dma((3,)),
+            dma((2,)),
             dma((4,)),
             dma((cuts,)),
             dma((4,)),
-            dma((3,)),
+            dma((2,)),
         ],
         compiler_params=pltpu.CompilerParams(
             collective_id=0, has_side_effects=True, vmem_limit_bytes=62000000

time: 85.8 us -> 86 us (level)
  no operation moved by 1% of the time
where the time goes in v3:
time: 86 us; the launch traced here: 85.8 us
  Pallas kernels  85 us (99%)
    pallas_call x1, Pallas kernels, fused(): pl.pallas_call(block_kernel, out_shape=pltpu.VMEM((rows, width), BF16), i...  85 us

profile of v3, /device:TPU:0, one launch (start us, length us, event | category | flops | bytes accessed | tf_op | source)
XLA Modules:
  0.0 85.8 jit_solution(1121964659423357258)
XLA Ops:
  0.0 85.0 %mlp_block.1 = bf16[64,4608]{1,0:T(8,128)(2,1)S(1)} custom-call(bf16[64,4608]{1,0:T(8,128)(2,1)} %tokens_hbm.1, f32[36,128]{1,0:T(8,128)} %bitcast.4, bf16[1152,6144]{1,0:T(8,128)(2,1)} %w_in_hbm.1, f32[48,128]{1,0:T(8,128)} %bitcast.3, bf16[6144,1152]{1,0:T(8,128)(2,1)} %w_out_hbm.1, f32[9,128]{1,0:T(8,128)} %bitcast.5), custom_call_target="tpu_custom_call" | custom-call | tf_op jit(solution)/shard_map/mlp_block/pallas_call | solution.py:340
  85.0 0.8 copy.8

commit v4 on v2

--- a/solution.py
+++ b/solution.py
@@ -40,6 +40,7 @@
     r, c = lax.axis_index("row"), lax.axis_index("col")
     y, k = r // 2, r % 2
     partner, across, diagonal = 2 * y + (1 - k), 2 * (1 - y) + k, 2 * (1 - y) + (1 - k)
+    h = (k + y) % 2
     others = (2 * (1 - y), 2 * (1 - y) + 1, partner)
     rows, width = tokens.shape
     depth = w_in.shape[0]
@@ -140,7 +141,7 @@
 
     def cross(j, at, n):
         at = (at, flat(j))
-        return remote(ssend.at[at], srecv.at[at], send_sem.at[2], s_recv.at[order(TAKEN, j, n)], across)
+        return remote(ssend.at[at], srecv.at[at], send_sem.at[2], s_recv.at[order(TAKEN, j, n)], diagonal)
 
     def spread(j, i, which):
         held = hidden.at[which, cut(TAKEN, j, i), flat(j)]
@@ -170,7 +171,7 @@
             def one(t):
                 x = panel[flat(j), :]
                 psend[t, flat(j), :] = jnp.dot(
-                    x, w_in[:, columns(1 - k, t)], preferred_element_type=F32
+                    x, w_in[:, columns(1 - h, t)], preferred_element_type=F32
                 ).astype(BF16)
 
             with scope(f"theirs{j}"):
@@ -183,7 +184,7 @@
 
             def one(t):
                 x = panel[flat(j), :]
-                mine = jnp.dot(x, w_in[:, columns(k, t)], preferred_element_type=F32)
+                mine = jnp.dot(x, w_in[:, columns(h, t)], preferred_element_type=F32)
                 ssend[t, flat(j), :] = (mine + precv[t, flat(j), :].astype(F32)).astype(BF16)
 
             with scope(f"ours{j}"):
@@ -212,8 +213,8 @@
 
         def theirs(i):
             with scope(f"spreadwait{j}"):
-                spread(j, i, 1 - k).wait_recv()
-            down(i, 1 - k)
+                spread(j, i, 1 - h).wait_recv()
+            down(i, 1 - h)
 
         for i in range(count):
             with scope(f"crosswait{j}"):
@@ -222,14 +223,14 @@
             def activate(t):
                 bias = b_in[:, pl.ds(pl.multiple_of(t * tile, tile), tile)]
                 v = ssend[t, flat(j), :].astype(F32) + srecv[t, flat(j), :].astype(F32) + bias
-                hidden[k, t, flat(j), :] = (v * (1.0 + lax.erf(v * (0.5**0.5))) * 0.5).astype(BF16)
+                hidden[h, t, flat(j), :] = (v * (1.0 + lax.erf(v * (0.5**0.5))) * 0.5).astype(BF16)
 
             with scope(f"gelu{j}"):
                 each_tile(TAKEN, j, i, activate)
-            spread(j, i, k).start()
+            spread(j, i, h).start()
             if j == 0 and i == 0:
                 load(1).wait()
-            down(i, k)
+            down(i, h)
             if i > 0:
                 theirs(i - 1)
         theirs(count - 1)
@@ -295,7 +296,7 @@
 
     vector(1).wait()
     vector(2).start()
-    flatten(b_in_ref, b_in, k * (half // 128), half)
+    flatten(b_in_ref, b_in, h * (half // 128), half)
     second(0)
     second(1)
     vector(2).wait()

time: 85.8 us -> 85.6 us (level)
  no operation moved by 1% of the time
where the time goes in v4:
time: 85.6 us; the launch traced here: 85.4 us
  Pallas kernels  84.6 us (99%)
    pallas_call x1, Pallas kernels, fused(): pl.pallas_call(block_kernel, out_shape=pltpu.VMEM((rows, width), BF16), i...  84.6 us

profile of v4, /device:TPU:0, one launch (start us, length us, event | category | flops | bytes accessed | tf_op | source)
XLA Modules:
  0.0 85.4 jit_solution(11832726546835105694)
XLA Ops:
  0.0 84.6 %mlp_block.1 = bf16[64,4608]{1,0:T(8,128)(2,1)S(1)} custom-call(bf16[64,4608]{1,0:T(8,128)(2,1)} %tokens_hbm.1, f32[36,128]{1,0:T(8,128)} %bitcast.4, bf16[1152,6144]{1,0:T(8,128)(2,1)} %w_in_hbm.1, f32[48,128]{1,0:T(8,128)} %bitcast.3, bf16[6144,1152]{1,0:T(8,128)(2,1)} %w_out_hbm.1, f32[9,128]{1,0:T(8,128)} %bitcast.5), custom_call_target="tpu_custom_call" | custom-call | tf_op jit(solution)/shard_map/mlp_block/pallas_call | solution.py:340
  84.6 0.8 copy.8
